TPU v7x, 32 devices: a whole 2x2x4 slice. The times are simulated.
32 devices in a mesh: side: 4 (over z), rep: 8 (over y, x, core).
Axes of the slice: x: 2, y: 2, z: 4, core: 2. Of those that a mesh axis runs over, the one named last changes fastest.
Arguments:
- w_up: float32 [4, 8, 1024, 1536], P('side', None, 'rep')
- w_down: float32 [4, 8, 1536, 1024], P('side', None, None, 'rep')
- g_up: float32 [4, 8, 1024, 1536], P('side', None, 'rep')
- g_down: float32 [4, 8, 1536, 1024], P('side', None, None, 'rep')
- learn_rate: float32 [], replicated
- prompts: bfloat16 [4, 16384, 512], P('side', 'rep')
- prompt_lens: int32 [8], P('rep')
Outputs:
- output 1: float32 [4, 8, 1024, 1536], P('side', None, 'rep')
- output 2: float32 [4, 8, 1536, 1024], P('side', None, None, 'rep')
- output 3: bfloat16 [4, 16384, 512], P('side', 'rep')
All inputs are finite; a program needn't handle non-finite values.
Results may differ from a plain program's by a relative error of at most 0.01907.
Values are sent between devices in bfloat16 or wider.
A program may use at most 1 GiB of HBM per device.

v0:
```python
import jax
import jax.numpy as jnp
from jax import lax
from jax.sharding import PartitionSpec as P


def solution(mesh):
    side_devs = mesh.shape["side"]
    tp_ways = side_devs // 2
    cross_perm = [(src_pos, src_pos + tp_ways) for src_pos in range(tp_ways)]
    up_spec = P("side", None, "rep", None)
    down_spec = P("side", None, None, "rep")
    act_spec = P("side", "rep", None)

    def device_step(w_up, w_down, g_up, g_down, learn_rate, prompts, prompt_lens):
        new_up = w_up - learn_rate * g_up
        new_down = w_down - learn_rate * g_down
        up_sent = lax.ppermute(new_up[0].astype(jnp.bfloat16), "side", cross_perm)
        down_sent = lax.ppermute(new_down[0].astype(jnp.bfloat16), "side", cross_perm)
        up_full = lax.all_gather(up_sent, "rep", axis=1, tiled=True)
        down_full = lax.all_gather(down_sent, "rep", axis=2, tiled=True)
        side_idx = lax.axis_index("side")
        is_gen = side_idx >= tp_ways
        tokens = prompts.shape[1]
        d_piece = prompts.shape[2]
        if tp_ways > 1:
            pieces = lax.all_gather(prompts[0], "side", axis=0)
            hidden = jnp.transpose(pieces[tp_ways:], (1, 0, 2)).reshape(tokens, tp_ways * d_piece)
        else:
            hidden = prompts[0]
        for layer_idx in range(up_full.shape[0]):
            pre_act = jnp.dot(hidden, up_full[layer_idx], preferred_element_type=jnp.float32)
            act_bf = jax.nn.gelu(pre_act, approximate=True).astype(jnp.bfloat16)
            part_sum = jnp.dot(act_bf, down_full[layer_idx], preferred_element_type=jnp.float32)
            if tp_ways > 1:
                part_sum = lax.psum(jnp.where(is_gen, part_sum, 0.0), "side")
            hidden = (hidden.astype(jnp.float32) + part_sum).astype(jnp.bfloat16)
        keep_mask = jnp.arange(tokens)[:, None] < prompt_lens[0]
        tp_idx = jnp.maximum(side_idx - tp_ways, 0)
        own_cols = lax.dynamic_slice_in_dim(hidden, tp_idx * d_piece, d_piece, axis=1)
        out_block = jnp.where(keep_mask & is_gen, own_cols, jnp.zeros_like(own_cols))
        return new_up, new_down, out_block[None]

    mapped = jax.shard_map(
        device_step,
        mesh=mesh,
        in_specs=(up_spec, down_spec, up_spec, down_spec, P(), act_spec, P("rep")),
        out_specs=(up_spec, down_spec, act_spec),
        check_vma=False,
    )
    return mapped
```

profile of v0, /device:TPU:0, one launch (start us, length us, event | category | flops | bytes accessed | tf_op | source)
XLA Modules:
  0.0 3162.8 jit_solution(10969436673993344579)
XLA Ops:
  23.1 135.5 %collective-permute-done.1 = bf16[8,1536,128]{2,1,0:T(8,128)(2,1)S(1)} collective-permute-done((bf16[8,1536,128]{2,1,0:T(8,128)(2,1)S(1)}, bf16[8,1536,128]{2,1,0:T(8,128)(2,1)S(1)}, u32[]{:S(2)}, u32[]{:S(2)}) %collective-permute-start.1) | collective-permute-done | bytes 3145760 | tf_op jit(solution)/shard_map/ppermute | solution.py:19
  160.3 8.9 convert_bitcast_fusion.1
  174.6 118.4 %collective-permute-done = bf16[8,128,1536]{2,1,0:T(8,128)(2,1)S(1)} collective-permute-done((bf16[8,128,1536]{2,1,0:T(8,128)(2,1)S(1)}, bf16[8,128,1536]{2,1,0:T(8,128)(2,1)S(1)}, u32[]{:S(2)}, u32[]{:S(2)}) %collective-permute-start) | collective-permute-done | bytes 3145760 | tf_op jit(solution)/shard_map/ppermute | solution.py:18
  300.2 193.7 %all-gather.8.cloned.1.call-done = bf16[8,1536,1024]{2,1,0:T(8,128)(2,1)} async-done(((bf16[8,1536,128]{2,1,0:T(8,128)(2,1)}), bf16[8,1536,1024]{2,1,0:T(8,128)(2,1)}) %all-gather.8.cloned.1.call-update) | async-done | bytes 25165840 | tf_op jit(solution)/shard_map/all_gather | solution.py:21
  494.0 127.1 %all-gather.6.cloned.1.call-done = bf16[8,1024,1536]{2,1,0:T(8,128)(2,1)} async-done(((bf16[8,128,1536]{2,1,0:T(8,128)(2,1)}), bf16[8,1024,1536]{2,1,0:T(8,128)(2,1)}) %all-gather.6.cloned.1.call-update) | async-done | bytes 25165840 | tf_op jit(solution)/shard_map/all_gather | solution.py:20
  621.1 22.2 broadcast_select_fusion.7
  643.4 288.8 %all-reduce.9.cloned.1.call-done = f32[2048,1024]{1,0:T(8,128)} async-done(((f32[2048,1024]{1,0:T(8,128)}), f32[2048,1024]{1,0:T(8,128)}) %all-reduce.9.cloned.1.call-update) | async-done | bytes 8388624 | tf_op jit(solution)/shard_map/psum | solution.py:36
  932.2 22.9 broadcast_select_fusion.6
  955.4 287.7 %all-reduce.11.cloned.1.call-done = f32[2048,1024]{1,0:T(8,128)} async-done(((f32[2048,1024]{1,0:T(8,128)}), f32[2048,1024]{1,0:T(8,128)}) %all-reduce.11.cloned.1.call-update) | async-done | bytes 8388624 | tf_op jit(solution)/shard_map/psum | solution.py:36
  1243.1 11.5 add_convert_fusion.5
  1254.6 23.2 broadcast_select_fusion.5
  1277.9 287.8 %all-reduce.13.cloned.1.call-done = f32[2048,1024]{1,0:T(8,128)} async-done(((f32[2048,1024]{1,0:T(8,128)}), f32[2048,1024]{1,0:T(8,128)}) %all-reduce.13.cloned.1.call-update) | async-done | bytes 8388624 | tf_op jit(solution)/shard_map/psum | solution.py:36
  1565.7 23.0 broadcast_select_fusion.4
  1589.0 287.7 %all-reduce.15.cloned.1.call-done = f32[2048,1024]{1,0:T(8,128)} async-done(((f32[2048,1024]{1,0:T(8,128)}), f32[2048,1024]{1,0:T(8,128)}) %all-reduce.15.cloned.1.call-update) | async-done | bytes 8388624 | tf_op jit(solution)/shard_map/psum | solution.py:36
  1876.6 11.5 add_convert_fusion.3
  1888.2 23.2 broadcast_select_fusion.3
  1911.5 287.8 %all-reduce.17.cloned.1.call-done = f32[2048,1024]{1,0:T(8,128)} async-done(((f32[2048,1024]{1,0:T(8,128)}), f32[2048,1024]{1,0:T(8,128)}) %all-reduce.17.cloned.1.call-update) | async-done | bytes 8388624 | tf_op jit(solution)/shard_map/psum | solution.py:36
  2199.3 22.9 broadcast_select_fusion.2
  2222.5 287.6 %all-reduce.19.cloned.1.call-done = f32[2048,1024]{1,0:T(8,128)} async-done(((f32[2048,1024]{1,0:T(8,128)}), f32[2048,1024]{1,0:T(8,128)}) %all-reduce.19.cloned.1.call-update) | async-done | bytes 8388624 | tf_op jit(solution)/shard_map/psum | solution.py:36
  2510.1 11.5 add_convert_fusion.1
  2521.6 23.1 broadcast_select_fusion.1
  2544.8 287.8 %all-reduce.21.cloned.1.call-done = f32[2048,1024]{1,0:T(8,128)} async-done(((f32[2048,1024]{1,0:T(8,128)}), f32[2048,1024]{1,0:T(8,128)}) %all-reduce.21.cloned.1.call-update) | async-done | bytes 8388624 | tf_op jit(solution)/shard_map/psum | solution.py:36
  2840.8 23.1 broadcast_select_fusion
  2864.6 287.2 %all-reduce.23.cloned.1.call-done = f32[2048,1024]{1,0:T(8,128)} async-done(((f32[2048,1024]{1,0:T(8,128)}), f32[2048,1024]{1,0:T(8,128)}) %all-reduce.23.cloned.1.call-update) | async-done | bytes 8388624 | tf_op jit(solution)/shard_map/psum | solution.py:36
  (35 shorter events, 42.7 us)
Async XLA Ops:
  7.2 287.9 %all-gather.4.cloned.1.call-start = ((), (), s32[]{:S(2)}) async-start(), calls=%async_computation | async-start | bytes 10485760 | tf_op jit(solution)/shard_map/all_gather | solution.py:27
  7.9 486.1 %all-gather.8.cloned.1.call-start = ((), (), s32[]{:S(2)}) async-start(), calls=%async_computation.2 | async-start | bytes 28311552 | tf_op jit(solution)/shard_map/all_gather | solution.py:21
  16.9 141.7 %collective-permute-start.1 = (bf16[8,1536,128]{2,1,0:T(8,128)(2,1)S(1)}, bf16[8,1536,128]{2,1,0:T(8,128)(2,1)S(1)}, u32[]{:S(2)}, u32[]{:S(2)}) collective-permute-start(bf16[8,1536,128]{2,1,0:T(8,128)(2,1)S(1)} %get-tuple-element.5), channel_id=1, source_target_pairs={{0,16},{8,24},{1,17},{9,25},{2,18},{10,26},{3,19},{11,27},{4,20},{... | collective-permute-start | bytes 9437192 | tf_op jit(solution)/shard_map/ppermute | solution.py:19
  158.6 1.7 copy-start
  160.2 460.9 %all-gather.6.cloned.1.call-start = ((), (), s32[]{:S(2)}) async-start(), calls=%async_computation.1 | async-start | bytes 28311552 | tf_op jit(solution)/shard_map/all_gather | solution.py:20
  169.1 123.9 %collective-permute-start = (bf16[8,128,1536]{2,1,0:T(8,128)(2,1)S(1)}, bf16[8,128,1536]{2,1,0:T(8,128)(2,1)S(1)}, u32[]{:S(2)}, u32[]{:S(2)}) collective-permute-start(bf16[8,128,1536]{2,1,0:T(8,128)(2,1)S(1)} %get-tuple-element.3), channel_id=1, source_target_pairs={{0,16},{8,24},{1,17},{9,25},{2,18},{10,26},{3,19},{11,27},{4,20},{... | collective-permute-start | bytes 9437192 | tf_op jit(solution)/shard_map/ppermute | solution.py:18
  293.1 1.7 copy-start.1
  294.8 637.4 %all-reduce.9.cloned.1.call-start = ((), (), s32[]{:S(2)}) async-start(), calls=%async_computation.3 | async-start | bytes 16777216 | tf_op jit(solution)/shard_map/psum | solution.py:36
  643.3 599.7 %all-reduce.11.cloned.1.call-start = ((), (), s32[]{:S(2)}) async-start(), calls=%async_computation.4 | async-start | bytes 16777216 | tf_op jit(solution)/shard_map/psum | solution.py:36
  955.2 610.5 %all-reduce.13.cloned.1.call-start = ((), (), s32[]{:S(2)}) async-start(), calls=%async_computation.5 | async-start | bytes 16777216 | tf_op jit(solution)/shard_map/psum | solution.py:36
  1277.8 598.8 %all-reduce.15.cloned.1.call-start = ((), (), s32[]{:S(2)}) async-start(), calls=%async_computation.6 | async-start | bytes 16777216 | tf_op jit(solution)/shard_map/psum | solution.py:36
  1588.8 610.5 %all-reduce.17.cloned.1.call-start = ((), (), s32[]{:S(2)}) async-start(), calls=%async_computation.7 | async-start | bytes 16777216 | tf_op jit(solution)/shard_map/psum | solution.py:36
  1911.4 598.7 %all-reduce.19.cloned.1.call-start = ((), (), s32[]{:S(2)}) async-start(), calls=%async_computation.8 | async-start | bytes 16777216 | tf_op jit(solution)/shard_map/psum | solution.py:36
  2222.3 610.4 %all-reduce.21.cloned.1.call-start = ((), (), s32[]{:S(2)}) async-start(), calls=%async_computation.9 | async-start | bytes 16777216 | tf_op jit(solution)/shard_map/psum | solution.py:36
  2544.7 607.0 %all-reduce.23.cloned.1.call-start = ((), (), s32[]{:S(2)}) async-start(), calls=%async_computation.10 | async-start | bytes 16777216 | tf_op jit(solution)/shard_map/psum | solution.py:36
Sparse Core Ops, SparseCore 0:
  9.5 267.3 all-gather.3
  278.8 215.0 all-gather.7
  495.9 125.1 all-gather.5
  643.5 288.7 all-reduce.8
  955.3 287.7 all-reduce.10
  1278.0 287.7 all-reduce.12
  1588.9 287.7 all-reduce.14
  1911.5 287.7 all-reduce.16
  2222.4 287.7 all-reduce.18
  2544.9 287.7 all-reduce.20
  2864.0 287.7 all-reduce.22
where the time goes:
time: 3170 us; the launch traced here: 3160 us
  waiting for transfers between devices  2880 us (91%)
  matrix products  184 us (6%)
  other arithmetic  63.9 us (2%)
    psum x8, waiting for transfers between devices, device_step(): part_sum = lax.psum(jnp.where(is_gen, part_sum, 0.0), 'side')  2300 us
    all_gather x1, waiting for transfers between devices, device_step(): down_full = lax.all_gather(down_sent, 'rep', axis=2, tiled=True)  194 us
    dot_general x8, matrix products, device_step(): jnp.dot(act_bf, down_full[layer_idx], preferred_element_type=jnp.float32)  184 us
    ppermute x1, waiting for transfers between devices, device_step(): lax.ppermute(new_down[0].astype(jnp.bfloat16), 'side', cross_perm)  135 us
    all_gather x1, waiting for transfers between devices, device_step(): up_full = lax.all_gather(up_sent, 'rep', axis=1, tiled=True)  127 us
    ppermute x1, waiting for transfers between devices, device_step(): up_sent = lax.ppermute(new_up[0].astype(jnp.bfloat16), 'side', cross_perm)  118 us
  transfers between devices with their start and end apart: 13, of which 12 were waited for; matrix products, arithmetic and copies ran while one was open for 1% of the time, Pallas kernels for 0%

commit v1 on v0

v1 whole, which is shorter than its diff:
```python
import functools

import jax
import jax.numpy as jnp
from jax import lax
from jax.experimental import pallas as pl
from jax.experimental.pallas import tpu as pltpu
from jax.sharding import PartitionSpec as P

MESH = pl.DeviceIdType.MESH
PLANES = 4
REPS = 8


def _gelu(z):
    inner = 0.7978845608028654 * (z + 0.044715 * (z * z * z))
    return z * (0.5 * (1.0 + jnp.tanh(inner)))


def _pipeline_kernel(
    upb, dnb, x_ref, y_ref,
    wu, wd, hin, hout, mid, act,
    z_recv, z_send, x_recv, x_send, y_recv, y_send, d_recv, d_send, s_recv, s_send,
    in_recv, in_send, h_recv, h_send, out_recv, out_send, out_loc,
    *, chunk, tile_n, tile_m,
):
    z = lax.axis_index("side")
    r = lax.axis_index("rep")
    core = r % 2
    xpos = (r // 2) % 2
    ypos = r // 4
    r_x = r + 2 - 4 * xpos
    r_y = r + 4 - 8 * ypos
    r_d = r_x + 4 - 8 * ypos
    r_s = r + 1 - 2 * core

    width = upb.shape[1]
    ff = upb.shape[2]
    tokens, d_half = x_ref.shape
    n_chunks = tokens // chunk
    first_rank = jnp.minimum(z, 1)

    def dev(zz, rr):
        return (zz, rr)

    barrier = pltpu.get_barrier_semaphore()
    for step in range(1, PLANES):
        pl.semaphore_signal(barrier, inc=1, device_id=dev((z + step) % PLANES, r), device_id_type=MESH)
    for rr in (r_x, r_y, r_s):
        pl.semaphore_signal(barrier, inc=1, device_id=dev(z, rr), device_id_type=MESH)
    pl.semaphore_wait(barrier, PLANES + 2)

    def remote(src, dst, send, recv, to):
        return pltpu.make_async_remote_copy(
            src_ref=src, dst_ref=dst, send_sem=send, recv_sem=recv, device_id=to, device_id_type=MESH)

    def piece(jk, rank, rr):
        j, k = jk // 2, jk % 2
        off = pl.multiple_of(rr * width, width)
        if isinstance(rank, int):
            hid = pl.ds(rank * ff, ff)
        else:
            hid = pl.ds(pl.multiple_of(rank * ff, ff), ff)
        if k == 0:
            return wu.at[j, pl.ds(off, width), hid]
        return wd.at[j, hid, pl.ds(off, width)]

    def shard(jk, plane):
        src = upb if jk % 2 == 0 else dnb
        return src.at[2 * plane + jk // 2]

    def prompt_copy(i):
        rows = pl.ds(pl.multiple_of(i * chunk, chunk), chunk)
        half = jnp.maximum(z - 2, 0)
        cols = pl.ds(pl.multiple_of(half * d_half, d_half), d_half)
        return remote(x_ref.at[rows, :], hin.at[rows, cols], in_send.at[i],
                      in_recv.at[half * n_chunks + i], dev(0, r))

    @pl.when(z >= 2)
    def _():
        def body(i, carry):
            prompt_copy(i).start()
            return carry
        lax.fori_loop(0, n_chunks, body, 0)

    def weight_copy(rank, plane, jk):
        e = jk if rank == min(plane, 1) else jk + 4
        if plane == rank:
            return pltpu.make_async_copy(shard(jk, plane), piece(jk, rank, r), z_recv.at[e])
        return remote(shard(jk, plane), piece(jk, rank, r), z_send.at[plane * 4 + jk],
                      z_recv.at[e], dev(plane, r))

    for rank in range(2):
        @pl.when(z == rank)
        def _():
            for plane in [rank] + [p for p in range(PLANES) if p != rank]:
                for jk in range(4):
                    weight_copy(rank, plane, jk).start()

    def rank_of(e):
        return first_rank if e < 4 else 1 - first_rank

    def spread(e, kind):
        jk = e % 4
        own = piece(jk, rank_of(e), r)
        if kind == "x":
            return remote(own, own, x_send.at[e], x_recv.at[e], dev(z, r_x))
        return remote(own, own, y_send.at[e], y_recv.at[e], dev(z, r_y))

    def relay(e):
        jk = e % 4
        if jk % 2 == 0:
            ref, to = piece(jk, rank_of(e), r_x), r_y
        else:
            ref, to = piece(jk, rank_of(e), r_y), r_x
        return remote(ref, ref, d_send.at[e], d_recv.at[e], dev(z, to))

    def to_sibling(e, q):
        ref = piece(e % 4, rank_of(e), (r, r_x, r_y, r_d)[q])
        return remote(ref, ref, s_send.at[q * 8 + e], s_recv.at[q * 8 + e], dev(z, r_s))

    def from_sibling(e, q):
        flip = 1 - 2 * core
        ref = piece(e % 4, rank_of(e), (r, r_x, r_y, r_d)[q] + flip)
        return remote(ref, ref, s_send.at[q * 8 + e], s_recv.at[q * 8 + e], dev(z, r_s))

    def landed(ref, sem):
        remote(ref, ref, sem, sem, dev(z, r_s)).wait_recv()

    for i in range(8 + 4):
        if i < 8:
            landed(piece(i % 4, rank_of(i), r), z_recv.at[i])
            spread(i, "x").start()
            spread(i, "y").start()
            to_sibling(i, 0).start()
        if 0 <= i - 2 < 8:
            e = i - 2
            landed(piece(e % 4, rank_of(e), r_x), x_recv.at[e])
            if e % 2 == 0:
                relay(e).start()
            landed(piece(e % 4, rank_of(e), r_y), y_recv.at[e])
            if e % 2 == 1:
                relay(e).start()
            to_sibling(e, 1).start()
            to_sibling(e, 2).start()
        if 0 <= i - 4 < 8:
            e = i - 4
            landed(piece(e % 4, rank_of(e), r_d), d_recv.at[e])
            to_sibling(e, 3).start()
    for e in range(8):
        for q in range(4):
            from_sibling(e, q).wait_recv()

    hidden = wu.shape[2]
    model = wu.shape[1]

    def hop_copy(i):
        rows = pl.ds(pl.multiple_of(i * chunk, chunk), chunk)
        return remote(hout.at[rows, :], hin.at[rows, :], h_send.at[i], h_recv.at[i],
                      dev(jnp.minimum(z + 1, PLANES - 1), r))

    def out_remote(i):
        rows = pl.ds(pl.multiple_of(i * chunk, chunk), chunk)
        return remote(hout.at[rows, pl.ds(0, d_half)], y_ref.at[rows, :], out_send.at[i], out_recv.at[i], dev(2, r))

    def out_local(i):
        rows = pl.ds(pl.multiple_of(i * chunk, chunk), chunk)
        return pltpu.make_async_copy(hout.at[rows, pl.ds(d_half, d_half)], y_ref.at[rows, :], out_loc.at[i])

    def layer(j, src, src_rows, dst, dst_rows):
        for n in range(hidden // tile_n):
            cols = pl.ds(n * tile_n, tile_n)
            pre = jnp.dot(src[src_rows, :], wu[j, :, cols], preferred_element_type=jnp.float32)
            act[:, cols] = _gelu(pre).astype(jnp.bfloat16)
        for m in range(model // tile_m):
            cols = pl.ds(m * tile_m, tile_m)
            part = jnp.dot(act[...], wd[j, :, cols], preferred_element_type=jnp.float32)
            dst[dst_rows, cols] = (src[src_rows, cols].astype(jnp.float32) + part).astype(jnp.bfloat16)

    def chunk_step(i, carry):
        rows = pl.ds(pl.multiple_of(i * chunk, chunk), chunk)

        @pl.when(z == 0)
        def _():
            for half in range(2):
                landed(hin.at[rows, pl.ds(half * d_half, d_half)], in_recv.at[half * n_chunks + i])

        @pl.when(z > 0)
        def _():
            landed(hin.at[rows, :], h_recv.at[i])

        layer(0, hin, rows, mid, pl.ds(0, chunk))
        layer(1, mid, pl.ds(0, chunk), hout, rows)

        @pl.when(z < PLANES - 1)
        def _():
            hop_copy(i).start()

        @pl.when(z == PLANES - 1)
        def _():
            out_remote(i).start()
            out_local(i).start()

        return carry

    lax.fori_loop(0, n_chunks, chunk_step, 0)

    def drain(fn):
        def body(i, carry):
            fn(i)
            return carry
        lax.fori_loop(0, n_chunks, body, 0)

    @pl.when(z >= 2)
    def _():
        drain(lambda i: prompt_copy(i).wait_send())

    for rank in range(2):
        @pl.when(z == rank)
        def _():
            for plane in range(PLANES):
                if plane != rank:
                    for jk in range(4):
                        weight_copy(rank, plane, jk).wait_send()

    for e in range(8):
        spread(e, "x").wait_send()
        spread(e, "y").wait_send()
        relay(e).wait_send()
        for q in range(4):
            to_sibling(e, q).wait_send()

    @pl.when(z < PLANES - 1)
    def _():
        drain(lambda i: hop_copy(i).wait_send())

    @pl.when(z == PLANES - 1)
    def _():
        drain(lambda i: out_remote(i).wait_send())
        drain(lambda i: out_local(i).wait())

    @pl.when(z == 2)
    def _():
        drain(lambda i: out_remote(i).wait_recv())


def solution(mesh):
    side_devs = mesh.shape["side"]
    tp_ways = side_devs // 2
    up_spec = P("side", None, "rep", None)
    down_spec = P("side", None, None, "rep")
    act_spec = P("side", "rep", None)

    def device_step(w_up, w_down, g_up, g_down, learn_rate, prompts, prompt_lens):
        new_up = w_up - learn_rate * g_up
        new_down = w_down - learn_rate * g_down
        upb = new_up[0].astype(jnp.bfloat16)
        dnb = new_down[0].astype(jnp.bfloat16)
        layers, width, ff = upb.shape
        tokens, d_half = prompts.shape[1:]
        model, hidden = width * REPS, ff * tp_ways
        chunk = min(256, tokens // 4)
        n_chunks = tokens // chunk
        dma = pltpu.SemaphoreType.DMA
        hbm = pl.BlockSpec(memory_space=pltpu.HBM)
        y = pl.pallas_call(
            functools.partial(_pipeline_kernel, chunk=chunk, tile_n=min(512, ff), tile_m=min(512, d_half)),
            out_shape=jax.ShapeDtypeStruct((tokens, d_half), jnp.bfloat16),
            in_specs=[hbm, hbm, hbm],
            out_specs=hbm,
            scratch_shapes=[
                pltpu.VMEM((2, model, hidden), jnp.bfloat16),
                pltpu.VMEM((2, hidden, model), jnp.bfloat16),
                pltpu.VMEM((tokens, model), jnp.bfloat16),
                pltpu.VMEM((tokens, model), jnp.bfloat16),
                pltpu.VMEM((chunk, model), jnp.bfloat16),
                pltpu.VMEM((chunk, hidden), jnp.bfloat16),
                dma((8,)), dma((16,)), dma((8,)), dma((8,)), dma((8,)), dma((8,)),
                dma((8,)), dma((8,)), dma((32,)), dma((32,)),
                dma((2 * n_chunks,)), dma((n_chunks,)), dma((n_chunks,)), dma((n_chunks,)),
                dma((n_chunks,)), dma((n_chunks,)), dma((n_chunks,)),
            ],
            compiler_params=pltpu.CompilerParams(
                collective_id=0, has_side_effects=True, vmem_limit_bytes=60 * 1024 * 1024),
            name="layer_pipeline",
        )(upb, dnb, prompts[0])
        side_idx = lax.axis_index("side")
        keep = (jnp.arange(tokens)[:, None] < prompt_lens[0]) & (side_idx >= tp_ways)
        out_block = jnp.where(keep, y, jnp.zeros_like(y))
        return new_up, new_down, out_block[None]

    return jax.shard_map(
        device_step,
        mesh=mesh,
        in_specs=(up_spec, down_spec, up_spec, down_spec, P(), act_spec, P("rep")),
        out_specs=(up_spec, down_spec, act_spec),
        check_vma=False,
    )
```

time: 3170 us -> 338 us (0.11)
  the two profiles are of different devices: /device:TPU:0 before, /device:TPU:16 now
where the time goes in v1:
time: 338 us
  Pallas kernels  318 us (94%)
  other arithmetic  17.9 us (5%)
    pallas_call x1, Pallas kernels, device_step(): pl.pallas_call(functools.partial(_pipeline_kernel, chunk=chunk, tile_n=mi...  318 us
    convert_element_type x1, other arithmetic, device_step(): upb = new_up[0].astype(jnp.bfloat16)  10.4 us

profile of v1, /device:TPU:16, one launch (start us, length us, event | category | flops | bytes accessed | tf_op | source)
XLA Modules:
  0.0 337.8 jit_solution(13821627165351763359)
XLA Ops:
  1.3 0.0 copy-start
  1.3 0.0 copy-start.1
  1.3 10.4 %convert_bitcast_fusion.1 = (bf16[8,128,1536]{2,1,0:T(8,128)(2,1)}, f32[1,8,128,1536]{3,2,1,0:T(8,128)}) fusion(f32[1,8,128,1536]{3,2,1,0:T(8,128)} %param.7, f32[1,8,128,1536]{3,2,1,0:T(8,128)} %param.9, f32[]{:T(128)S(6)} %copy.10), kind=kLoop, calls=%fused_computation.3 | loop fusion | flops 4718592 | bytes 22020100 | tf_op jit(solution)/shard_map/convert_element_type | solution.py:257
  11.7 0.0 copy-done
  11.7 0.0 copy-done.1
  11.7 4.7 %convert_bitcast_fusion = (bf16[8,1536,128]{2,1,0:T(8,128)(2,1)}, f32[1,8,1536,128]{3,2,1,0:T(8,128)}) fusion(f32[1,8,1536,128]{3,2,1,0:T(8,128)S(1)} %copy-done, f32[1,8,1536,128]{3,2,1,0:T(8,128)S(1)} %copy-done.1, f32[]{:T(128)S(6)} %copy.10), kind=kLoop, calls=%fused_computation.2 | loop fusion | flops 4718592 | bytes 22020100 | tf_op jit(solution)/shard_map/convert_element_type | solution.py:258
  16.4 318.0 %layer_pipeline.1 = bf16[2048,512]{1,0:T(8,128)(2,1)} custom-call(bf16[8,128,1536]{2,1,0:T(8,128)(2,1)} %get-tuple-element.5.upb, bf16[8,1536,128]{2,1,0:T(8,128)(2,1)} %get-tuple-element.3.dnb, bf16[2048,512]{1,0:T(8,128)(2,1)} %bitcast.9), custom_call_target="tpu_custom_call" | custom-call | tf_op jit(solution)/shard_map/layer_pipeline/pallas_call | solution.py:266
  335.1 2.8 select_bitcast_fusion
  (1 shorter events, 0.0 us)
Async XLA Ops:
  1.3 10.4 %copy-start = (f32[1,8,1536,128]{3,2,1,0:T(8,128)S(1)}, f32[1,8,1536,128]{3,2,1,0:T(8,128)}, u32[]{:S(2)}) copy-start(f32[1,8,1536,128]{3,2,1,0:T(8,128)} %param.8) | copy-start | bytes 18874372
  1.3 10.4 %copy-start.1 = (f32[1,8,1536,128]{3,2,1,0:T(8,128)S(1)}, f32[1,8,1536,128]{3,2,1,0:T(8,128)}, u32[]{:S(2)}) copy-start(f32[1,8,1536,128]{3,2,1,0:T(8,128)} %param.10) | copy-start | bytes 18874372

commit v2 on v1

--- a/solution.py
+++ b/solution.py
@@ -10,6 +10,7 @@
 MESH = pl.DeviceIdType.MESH
 PLANES = 4
 REPS = 8
+UNITS = ((0, 0), (0, 1), (0, 2), (1, 0), (0, 3), (1, 1), (1, 2), (1, 3))
 
 
 def _gelu(z):
@@ -37,18 +38,22 @@
     width = upb.shape[1]
     ff = upb.shape[2]
     tokens, d_half = x_ref.shape
-    n_chunks = tokens // chunk
     first_rank = jnp.minimum(z, 1)
+    n_big = tokens // chunk - 1
+    small = chunk // 2
+    n_chunks = n_big + 2
 
     def dev(zz, rr):
         return (zz, rr)
 
     barrier = pltpu.get_barrier_semaphore()
+    scope = jax.named_scope
     for step in range(1, PLANES):
         pl.semaphore_signal(barrier, inc=1, device_id=dev((z + step) % PLANES, r), device_id_type=MESH)
     for rr in (r_x, r_y, r_s):
         pl.semaphore_signal(barrier, inc=1, device_id=dev(z, rr), device_id_type=MESH)
-    pl.semaphore_wait(barrier, PLANES + 2)
+    with scope("entry"):
+        pl.semaphore_wait(barrier, PLANES + 2)
 
     def remote(src, dst, send, recv, to):
         return pltpu.make_async_remote_copy(
@@ -69,22 +74,28 @@
         src = upb if jk % 2 == 0 else dnb
         return src.at[2 * plane + jk // 2]
 
-    def prompt_copy(i):
-        rows = pl.ds(pl.multiple_of(i * chunk, chunk), chunk)
+    def big(i):
+        return pl.ds(pl.multiple_of(i * chunk, chunk), chunk)
+
+    def tail(i):
+        return pl.ds(n_big * chunk + (i - n_big) * small, small)
+
+    def prompt_copy(i, rows):
         half = jnp.maximum(z - 2, 0)
         cols = pl.ds(pl.multiple_of(half * d_half, d_half), d_half)
         return remote(x_ref.at[rows, :], hin.at[rows, cols], in_send.at[i],
                       in_recv.at[half * n_chunks + i], dev(0, r))
 
-    @pl.when(z >= 2)
-    def _():
+    def each_chunk(fn):
         def body(i, carry):
-            prompt_copy(i).start()
+            fn(i, big(i))
             return carry
-        lax.fori_loop(0, n_chunks, body, 0)
+        lax.fori_loop(0, n_big, body, 0)
+        for i in range(n_big, n_chunks):
+            fn(i, tail(i))
 
     def weight_copy(rank, plane, jk):
-        e = jk if rank == min(plane, 1) else jk + 4
+        e = UNITS.index((0 if rank == min(plane, 1) else 1, jk))
         if plane == rank:
             return pltpu.make_async_copy(shard(jk, plane), piece(jk, rank, r), z_recv.at[e])
         return remote(shard(jk, plane), piece(jk, rank, r), z_send.at[plane * 4 + jk],
@@ -93,92 +104,92 @@
     for rank in range(2):
         @pl.when(z == rank)
         def _():
-            for plane in [rank] + [p for p in range(PLANES) if p != rank]:
-                for jk in range(4):
-                    weight_copy(rank, plane, jk).start()
-
-    def rank_of(e):
-        return first_rank if e < 4 else 1 - first_rank
+            order = [(rank, jk) for jk in range(4)] + [(1 - rank, jk) for jk in range(4)]
+            order += [(plane, jk) for jk in range(4) for plane in (2, 3)]
+            for plane, jk in order:
+                weight_copy(rank, plane, jk).start()
+
+    def unit(e, rr):
+        late, jk = UNITS[e]
+        return piece(jk, 1 - first_rank if late else first_rank, rr)
 
     def spread(e, kind):
-        jk = e % 4
-        own = piece(jk, rank_of(e), r)
+        own = unit(e, r)
         if kind == "x":
             return remote(own, own, x_send.at[e], x_recv.at[e], dev(z, r_x))
         return remote(own, own, y_send.at[e], y_recv.at[e], dev(z, r_y))
 
     def relay(e):
-        jk = e % 4
-        if jk % 2 == 0:
-            ref, to = piece(jk, rank_of(e), r_x), r_y
+        if UNITS[e][1] % 2 == 0:
+            ref, to = unit(e, r_x), r_y
         else:
-            ref, to = piece(jk, rank_of(e), r_y), r_x
+            ref, to = unit(e, r_y), r_x
         return remote(ref, ref, d_send.at[e], d_recv.at[e], dev(z, to))
 
     def to_sibling(e, q):
-        ref = piece(e % 4, rank_of(e), (r, r_x, r_y, r_d)[q])
-        return remote(ref, ref, s_send.at[q * 8 + e], s_recv.at[q * 8 + e], dev(z, r_s))
-
-    def from_sibling(e, q):
-        flip = 1 - 2 * core
-        ref = piece(e % 4, rank_of(e), (r, r_x, r_y, r_d)[q] + flip)
+        ref = unit(e, (r, r_x, r_y, r_d)[q])
         return remote(ref, ref, s_send.at[q * 8 + e], s_recv.at[q * 8 + e], dev(z, r_s))
 
     def landed(ref, sem):
         remote(ref, ref, sem, sem, dev(z, r_s)).wait_recv()
 
+    def from_sibling(e, q):
+        landed(unit(e, (r, r_x, r_y, r_d)[q] + 1 - 2 * core), s_recv.at[q * 8 + e])
+
     for i in range(8 + 4):
+        if 0 <= i - 4:
+            e = i - 4
+            with scope(f"dw{e}"):
+                landed(unit(e, r_d), d_recv.at[e])
+            to_sibling(e, 3).start()
+        if 0 <= i - 2 < 8:
+            e = i - 2
+            with scope(f"xw{e}"):
+                landed(unit(e, r_x), x_recv.at[e])
+                landed(unit(e, r_y), y_recv.at[e])
+            relay(e).start()
+            to_sibling(e, 1).start()
+            to_sibling(e, 2).start()
         if i < 8:
-            landed(piece(i % 4, rank_of(i), r), z_recv.at[i])
+            with scope(f"zw{i}"):
+                landed(unit(i, r), z_recv.at[i])
             spread(i, "x").start()
             spread(i, "y").start()
             to_sibling(i, 0).start()
-        if 0 <= i - 2 < 8:
-            e = i - 2
-            landed(piece(e % 4, rank_of(e), r_x), x_recv.at[e])
-            if e % 2 == 0:
-                relay(e).start()
-            landed(piece(e % 4, rank_of(e), r_y), y_recv.at[e])
-            if e % 2 == 1:
-                relay(e).start()
-            to_sibling(e, 1).start()
-            to_sibling(e, 2).start()
-        if 0 <= i - 4 < 8:
-            e = i - 4
-            landed(piece(e % 4, rank_of(e), r_d), d_recv.at[e])
-            to_sibling(e, 3).start()
-    for e in range(8):
-        for q in range(4):
-            from_sibling(e, q).wait_recv()
+        if i == 1:
+            @pl.when(z >= 2)
+            def _():
+                each_chunk(lambda c, rows: prompt_copy(c, rows).start())
+    with scope("sib"):
+        for e in range(8):
+            for q in range(4):
+                from_sibling(e, q)
 
     hidden = wu.shape[2]
     model = wu.shape[1]
 
-    def hop_copy(i):
-        rows = pl.ds(pl.multiple_of(i * chunk, chunk), chunk)
+    def hop_copy(i, rows):
         return remote(hout.at[rows, :], hin.at[rows, :], h_send.at[i], h_recv.at[i],
                       dev(jnp.minimum(z + 1, PLANES - 1), r))
 
-    def out_remote(i):
-        rows = pl.ds(pl.multiple_of(i * chunk, chunk), chunk)
+    def out_remote(i, rows):
         return remote(hout.at[rows, pl.ds(0, d_half)], y_ref.at[rows, :], out_send.at[i], out_recv.at[i], dev(2, r))
 
-    def out_local(i):
-        rows = pl.ds(pl.multiple_of(i * chunk, chunk), chunk)
+    def out_local(i, rows):
         return pltpu.make_async_copy(hout.at[rows, pl.ds(d_half, d_half)], y_ref.at[rows, :], out_loc.at[i])
 
-    def layer(j, src, src_rows, dst, dst_rows):
+    def layer(j, src, src_rows, dst, dst_rows, size):
         for n in range(hidden // tile_n):
             cols = pl.ds(n * tile_n, tile_n)
             pre = jnp.dot(src[src_rows, :], wu[j, :, cols], preferred_element_type=jnp.float32)
-            act[:, cols] = _gelu(pre).astype(jnp.bfloat16)
+            act[:size, cols] = _gelu(pre).astype(jnp.bfloat16)
         for m in range(model // tile_m):
             cols = pl.ds(m * tile_m, tile_m)
-            part = jnp.dot(act[...], wd[j, :, cols], preferred_element_type=jnp.float32)
+            part = jnp.dot(act[:size, :], wd[j, :, cols], preferred_element_type=jnp.float32)
             dst[dst_rows, cols] = (src[src_rows, cols].astype(jnp.float32) + part).astype(jnp.bfloat16)
 
-    def chunk_step(i, carry):
-        rows = pl.ds(pl.multiple_of(i * chunk, chunk), chunk)
+    def chunk_step(i, rows):
+        size = rows.size
 
         @pl.when(z == 0)
         def _():
@@ -189,31 +200,33 @@
         def _():
             landed(hin.at[rows, :], h_recv.at[i])
 
-        layer(0, hin, rows, mid, pl.ds(0, chunk))
-        layer(1, mid, pl.ds(0, chunk), hout, rows)
+        with scope("layers"):
+            layer(0, hin, rows, mid, pl.ds(0, size), size)
+            layer(1, mid, pl.ds(0, size), hout, rows, size)
 
         @pl.when(z < PLANES - 1)
         def _():
-            hop_copy(i).start()
+            hop_copy(i, rows).start()
 
         @pl.when(z == PLANES - 1)
         def _():
-            out_remote(i).start()
-            out_local(i).start()
-
+            out_remote(i, rows).start()
+            out_local(i, rows).start()
+
+    def big_step(i, carry):
+        chunk_step(i, big(i))
         return carry
 
-    lax.fori_loop(0, n_chunks, chunk_step, 0)
-
-    def drain(fn):
-        def body(i, carry):
-            fn(i)
-            return carry
-        lax.fori_loop(0, n_chunks, body, 0)
+    def small_step(i, carry):
+        chunk_step(i, pl.ds(pl.multiple_of(n_big * chunk + (i - n_big) * small, small), small))
+        return carry
+
+    lax.fori_loop(0, n_big, big_step, 0)
+    lax.fori_loop(n_big, n_chunks, small_step, 0)
 
     @pl.when(z >= 2)
     def _():
-        drain(lambda i: prompt_copy(i).wait_send())
+        each_chunk(lambda i, rows: prompt_copy(i, rows).wait_send())
 
     for rank in range(2):
         @pl.when(z == rank)
@@ -232,16 +245,16 @@
 
     @pl.when(z < PLANES - 1)
     def _():
-        drain(lambda i: hop_copy(i).wait_send())
+        each_chunk(lambda i, rows: hop_copy(i, rows).wait_send())
 
     @pl.when(z == PLANES - 1)
     def _():
-        drain(lambda i: out_remote(i).wait_send())
-        drain(lambda i: out_local(i).wait())
+        each_chunk(lambda i, rows: out_remote(i, rows).wait_send())
+        each_chunk(lambda i, rows: out_local(i, rows).wait())
 
     @pl.when(z == 2)
     def _():
-        drain(lambda i: out_remote(i).wait_recv())
+        each_chunk(lambda i, rows: out_remote(i, rows).wait_recv())
 
 
 def solution(mesh):
@@ -260,7 +273,7 @@
         tokens, d_half = prompts.shape[1:]
         model, hidden = width * REPS, ff * tp_ways
         chunk = min(256, tokens // 4)
-        n_chunks = tokens // chunk
+        n_chunks = tokens // chunk + 1
         dma = pltpu.SemaphoreType.DMA
         hbm = pl.BlockSpec(memory_space=pltpu.HBM)
         y = pl.pallas_call(

time: 338 us -> 330 us (0.976)
  the two profiles are of different devices: /device:TPU:16 before, /device:TPU:17 now
where the time goes in v2:
time: 330 us
  Pallas kernels  310 us (94%)
  other arithmetic  17.9 us (5%)
    pallas_call x1, Pallas kernels, device_step(): pl.pallas_call(functools.partial(_pipeline_kernel, chunk=chunk, tile_n=mi...  310 us
    convert_element_type x1, other arithmetic, device_step(): upb = new_up[0].astype(jnp.bfloat16)  10.4 us

profile of v2, /device:TPU:17, one launch (start us, length us, event | category | flops | bytes accessed | tf_op | source)
XLA Modules:
  0.0 329.7 jit_solution(1446699847978798284)
XLA Ops:
  1.3 0.0 copy-start
  1.3 0.0 copy-start.1
  1.3 10.4 %convert_bitcast_fusion.1 = (bf16[8,128,1536]{2,1,0:T(8,128)(2,1)}, f32[1,8,128,1536]{3,2,1,0:T(8,128)}) fusion(f32[1,8,128,1536]{3,2,1,0:T(8,128)} %param.7, f32[1,8,128,1536]{3,2,1,0:T(8,128)} %param.9, f32[]{:T(128)S(6)} %copy.10), kind=kLoop, calls=%fused_computation.3 | loop fusion | flops 4718592 | bytes 22020100 | tf_op jit(solution)/shard_map/convert_element_type | solution.py:270
  11.7 0.0 copy-done
  11.7 0.0 copy-done.1
  11.7 4.7 %convert_bitcast_fusion = (bf16[8,1536,128]{2,1,0:T(8,128)(2,1)}, f32[1,8,1536,128]{3,2,1,0:T(8,128)}) fusion(f32[1,8,1536,128]{3,2,1,0:T(8,128)S(1)} %copy-done, f32[1,8,1536,128]{3,2,1,0:T(8,128)S(1)} %copy-done.1, f32[]{:T(128)S(6)} %copy.10), kind=kLoop, calls=%fused_computation.2 | loop fusion | flops 4718592 | bytes 22020100 | tf_op jit(solution)/shard_map/convert_element_type | solution.py:271
  16.4 309.8 %layer_pipeline.1 = bf16[2048,512]{1,0:T(8,128)(2,1)} custom-call(bf16[8,128,1536]{2,1,0:T(8,128)(2,1)} %get-tuple-element.5.upb, bf16[8,1536,128]{2,1,0:T(8,128)(2,1)} %get-tuple-element.3.dnb, bf16[2048,512]{1,0:T(8,128)(2,1)} %bitcast.9), custom_call_target="tpu_custom_call" | custom-call | tf_op jit(solution)/shard_map/layer_pipeline/pallas_call | solution.py:279
  326.9 2.8 select_bitcast_fusion
  (1 shorter events, 0.0 us)
Async XLA Ops:
  1.3 10.4 %copy-start = (f32[1,8,1536,128]{3,2,1,0:T(8,128)S(1)}, f32[1,8,1536,128]{3,2,1,0:T(8,128)}, u32[]{:S(2)}) copy-start(f32[1,8,1536,128]{3,2,1,0:T(8,128)} %param.8) | copy-start | bytes 18874372
  1.3 10.4 %copy-start.1 = (f32[1,8,1536,128]{3,2,1,0:T(8,128)S(1)}, f32[1,8,1536,128]{3,2,1,0:T(8,128)}, u32[]{:S(2)}) copy-start(f32[1,8,1536,128]{3,2,1,0:T(8,128)} %param.10) | copy-start | bytes 18874372
